TPU v7x, 32 devices: a whole 2x2x4 slice. The times are simulated.
32 devices in a mesh: img: 2 (over y), row: 8 (over z, x), col: 2 (over core).
Axes of the slice: x: 2, y: 2, z: 4, core: 2. Of those that a mesh axis runs over, the one named last changes fastest.
Arguments:
- features: bfloat16 [16, 128, 512], P(('img', 'row'), 'col'), parts along dimension 0, may hold values from -60 to 60
- first_gain: float32 [512], replicated, may hold values from 0.1 to 1.9
- first_shift: float32 [512], replicated, may hold values from -2.5 to 2.5
- first_weight: bfloat16 [3, 3, 512, 512], P(None, None, 'row'), may hold values from -0.09375 to 0.09375
- first_bias: float32 [512], replicated, may hold values from -2.5 to 2.5
- second_gain: float32 [512], replicated, may hold values from 0.1 to 1.9
- second_shift: float32 [512], replicated, may hold values from -2.5 to 2.5
- second_weight: bfloat16 [3, 3, 512, 512], P(None, None, 'row'), may hold values from -0.09375 to 0.09375
- second_bias: float32 [512], replicated, may hold values from -2.5 to 2.5
- upsample_weight: bfloat16 [3, 3, 512, 512], P(None, None, 'row'), may hold values from -0.09375 to 0.09375
- upsample_bias: float32 [512], replicated, may hold values from -2.5 to 2.5
Outputs:
- upsampled: bfloat16 [32, 256, 512], P(('img', 'row'), 'col'), parts along dimension 0
There are 2 independent parts, one for each index of `img`. A program takes and returns all parts, laid end to end along the dimension named above; an argument that names none is the same for every part. Nothing has to cross between parts.
All inputs are finite; a program needn't handle non-finite values.
Results may differ from a plain program's by a relative error of at most 0.0075.
Values may be sent and summed in bfloat16 or wider, within the bound.
A program may use at most 128 MiB of HBM per device.

v0:
```python
import jax
import jax.numpy as jnp
from jax import lax
from jax.sharding import PartitionSpec as P

G = 32
EPS = 1e-06


def extended(cells, sides, width):
    for axis, dim in sides:
        count = lax.axis_size(axis)
        ends = count - 1
        head = lax.slice_in_dim(cells, 0, width, axis=dim)
        tail = lax.slice_in_dim(cells, cells.shape[dim] - width, cells.shape[dim], axis=dim)
        cells = jnp.concatenate(
            [
                lax.ppermute(tail, axis, [(i, (i + 1) % count) for i in range(ends)]),
                cells,
                lax.ppermute(head, axis, [((i + 1) % count, i) for i in range(ends)]),
            ],
            axis=dim,
        )
    return cells


def norm_silu(values, gain, shift):
    height, breadth, channels = values.shape
    grouped = values.reshape(height * breadth, G, channels // G)
    total = jnp.sum(grouped, axis=(0, 2))
    squares = jnp.sum(grouped * grouped, axis=(0, 2))
    total, squares = lax.psum((total, squares), ("row", "col"))
    count = height * breadth * lax.axis_size("row") * lax.axis_size("col") * (channels // G)
    mean = total / count
    var = squares / count - mean * mean
    factor = lax.rsqrt(var + EPS)
    normed = (grouped - mean[None, :, None]) * factor[None, :, None]
    normed = normed.reshape(height, breadth, channels) * gain + shift
    return jax.nn.silu(normed).astype(jnp.bfloat16)


def extend(values):
    return extended(values, (("row", 0), ("col", 1)), 1)


def convolve(padded, weight, bias, height, breadth):
    outputs = weight.shape[3]
    empty = jnp.zeros((height, breadth, outputs), jnp.float32)
    share = weight.shape[2] // lax.axis_size("col")
    own = lax.dynamic_slice_in_dim(weight, lax.axis_index("col") * share, share, 2)
    total = empty
    piece = lax.all_gather(own, ("row", "col"), axis=2, tiled=True)
    depth = piece.shape[2]
    offset = jnp.asarray(jnp.int32(0), jnp.int32)
    for offset_y in range(3):
        for offset_x in range(3):
            window = lax.dynamic_slice(
                padded, (jnp.int32(offset_y), jnp.int32(offset_x), offset), (height, breadth, depth)
            )
            total = total + jnp.einsum(
                "hwk,kc->hwc", window, piece[offset_y, offset_x], preferred_element_type=jnp.float32
            )
    return total + bias


def on_device(
    features,
    first_gain,
    first_shift,
    first_weight,
    first_bias,
    second_gain,
    second_shift,
    second_weight,
    second_bias,
    upsample_weight,
    upsample_bias,
):
    height, breadth, channels = features.shape
    normed_one = norm_silu(features.astype(jnp.float32), first_gain, first_shift)
    hidden = convolve(extend(normed_one), first_weight, first_bias, height, breadth).astype(
        jnp.bfloat16
    )
    normed_two = norm_silu(hidden.astype(jnp.float32), second_gain, second_shift)
    block_out = (
        convolve(extend(normed_two), second_weight, second_bias, height, breadth)
        + features.astype(jnp.float32)
    ).astype(jnp.bfloat16)
    doubled = jnp.repeat(jnp.repeat(block_out, 2, axis=0), 2, axis=1)
    padded = extend(doubled)
    return convolve(padded, upsample_weight, upsample_bias, 2 * height, 2 * breadth).astype(
        jnp.bfloat16
    )


def solution(mesh):
    return jax.shard_map(
        on_device,
        mesh=mesh,
        in_specs=(
            P(("img", "row"), "col", None),
            P(),
            P(),
            P(None, None, "row", None),
            P(),
            P(),
            P(),
            P(None, None, "row", None),
            P(),
            P(None, None, "row", None),
            P(),
        ),
        out_specs=P(("img", "row"), "col", None),
        check_vma=False,
    )
```

profile of v0, /device:TPU:1, one launch (start us, length us, event | category | flops | bytes accessed | tf_op | source)
XLA Modules:
  0.0 196.7 jit_solution(13874195632810738690)
XLA Ops:
  6.5 1.1 copy-done
  7.6 0.8 constant_dynamic-slice_fusion.2
  8.4 1.7 constant_dynamic-slice_fusion.1
  10.2 1.7 constant_dynamic-slice_fusion
  12.0 0.9 convert_reduce_fusion
  13.2 31.1 %all-reduce.1 = (f32[32]{0:T(128)S(1)}, f32[32]{0:T(128)S(1)}) all-reduce(f32[32]{0:T(128)S(1)} %reduce_sum.54, f32[32]{0:T(128)S(1)} %reduce_sum.51), channel_id=1, replica_groups=mesh['img'=2,'row'=8,'col'=2] {'row','col'}, use_global_device_ids=true, to_apply=%region_5.6 | all-reduce | flops 64 | bytes 512 | tf_op jit(solution)/shard_map/psum | solution.py:32
  44.7 0.9 fusion.69
  45.6 1.3 collective-permute-start
  46.9 1.3 collective-permute-start.1
  48.2 1.8 collective-permute-done
  50.0 3.9 %collective-permute-done.1 = bf16[1,64,512]{2,1,0:T(8,128)(2,1)S(1)} collective-permute-done((bf16[1,64,512]{2,1,0:T(8,128)(2,1)S(1)}, bf16[1,64,512]{2,1,0:T(8,128)(2,1)S(1)}, u32[]{:S(2)}, u32[]{:S(2)}) %collective-permute-start.1) | collective-permute-done | bytes 65568 | tf_op jit(solution)/shard_map/ppermute | solution.py:20
  53.9 1.3 collective-permute-start.2
  55.2 5.6 %collective-permute-start.3 = (bf16[3,1,512]{2,1,0:T(2,128)(2,1)S(1)}, bf16[3,1,512]{2,1,0:T(2,128)(2,1)S(1)}, u32[]{:S(2)}, u32[]{:S(2)}) collective-permute-start(bf16[3,1,512]{2,1,0:T(2,128)(2,1)S(1)} %get-tuple-element.20), channel_id=1, source_target_pairs={{1,0},{3,2},{5,4},{7,6},{9,8},{11,10},{13,12},{15,14},{17,16},{19,... | collective-permute-start | bytes 9224 | tf_op jit(solution)/shard_map/ppermute | solution.py:20
  60.7 7.4 %all-gather.4.cloned.1.call-done = bf16[3,3,512,512]{3,2,1,0:T(8,128)(2,1)} async-done(((bf16[3,3,32,512]{3,2,1,0:T(8,128)(2,1)}), bf16[3,3,512,512]{3,2,1,0:T(8,128)(2,1)}) %all-gather.4.cloned.1.call-update) | async-done | bytes 4718608 | tf_op jit(solution)/shard_map/all_gather | solution.py:52
  68.1 1.2 fusion.46
  69.4 1.2 fusion.44
  70.6 1.2 fusion.47
  71.9 1.2 fusion.42
  73.1 1.2 fusion.48
  74.4 1.2 fusion.45
  75.6 1.3 fusion.43
  76.9 1.3 fusion.19
  78.2 1.3 fusion.151
  79.9 30.2 %all-reduce = (f32[32]{0:T(128)S(1)}, f32[32]{0:T(128)S(1)}) all-reduce(f32[32]{0:T(128)S(1)} %reduce_sum.75, f32[32]{0:T(128)S(1)} %reduce_sum.72), channel_id=1, replica_groups=mesh['img'=2,'row'=8,'col'=2] {'row','col'}, use_global_device_ids=true, to_apply=%region_11.12 | all-reduce | flops 64 | bytes 512 | tf_op jit(solution)/shard_map/psum | solution.py:32
  110.5 1.3 collective-permute-start.4
  111.8 1.3 collective-permute-start.5
  113.1 10.3 %all-gather.6.cloned.1.call-done = bf16[3,3,512,512]{3,2,1,0:T(8,128)(2,1)} async-done(((bf16[3,3,32,512]{3,2,1,0:T(8,128)(2,1)}), bf16[3,3,512,512]{3,2,1,0:T(8,128)(2,1)}) %all-gather.6.cloned.1.call-update) | async-done | bytes 4718608 | tf_op jit(solution)/shard_map/all_gather | solution.py:52
  123.4 1.2 fusion.38
  124.7 2.2 %collective-permute-start.7 = (bf16[3,1,512]{2,1,0:T(2,128)(2,1)S(1)}, bf16[3,1,512]{2,1,0:T(2,128)(2,1)S(1)}, u32[]{:S(2)}, u32[]{:S(2)}) collective-permute-start(bf16[3,1,512]{2,1,0:T(2,128)(2,1)S(1)} %get-tuple-element.18), channel_id=1, source_target_pairs={{1,0},{3,2},{5,4},{7,6},{9,8},{11,10},{13,12},{15,14},{17,16},{19,... | collective-permute-start | bytes 9224 | tf_op jit(solution)/shard_map/ppermute | solution.py:20
  126.9 1.3 collective-permute-start.6
  128.2 1.2 fusion.41
  129.4 1.2 fusion.36
  130.7 1.3 fusion.39
  132.0 1.3 fusion.37
  133.3 1.2 fusion.40
  134.5 1.2 fusion.35
  135.8 1.3 fusion.13
  137.1 1.3 fusion.27
  138.5 2.4 %collective-permute-start.8 = (bf16[1,128,512]{2,1,0:T(8,128)(2,1)S(1)}, bf16[1,128,512]{2,1,0:T(8,128)(2,1)S(1)}, u32[]{:S(2)}, u32[]{:S(2)}) collective-permute-start(bf16[1,128,512]{2,1,0:T(8,128)(2,1)S(1)} %slice.150), channel_id=1, source_target_pairs={{0,2},{2,4},{4,6},{6,8},{8,10},{10,12},{12,14},{1,3},{3,5},{5,7},{... | collective-permute-start | bytes 393224 | tf_op jit(solution)/shard_map/ppermute | solution.py:18
  140.9 1.3 collective-permute-start.9
  142.2 36.5 %all-gather.8.cloned.1.call-done = bf16[3,3,512,512]{3,2,1,0:T(8,128)(2,1)} async-done(((bf16[3,3,32,512]{3,2,1,0:T(8,128)(2,1)}), bf16[3,3,512,512]{3,2,1,0:T(8,128)(2,1)}) %all-gather.8.cloned.1.call-update) | async-done | bytes 4718608 | tf_op jit(solution)/shard_map/all_gather | solution.py:52
  178.8 1.5 fusion.31
  180.3 1.3 collective-permute-start.10
  181.6 3.0 %collective-permute-start.11 = (bf16[4,1,512]{2,1,0:T(2,128)(2,1)S(1)}, bf16[4,1,512]{2,1,0:T(2,128)(2,1)S(1)}, u32[]{:S(2)}, u32[]{:S(2)}) collective-permute-start(bf16[4,1,512]{2,1,0:T(2,128)(2,1)S(1)} %get-tuple-element.16), channel_id=1, source_target_pairs={{1,0},{3,2},{5,4},{7,6},{9,8},{11,10},{13,12},{15,14},{17,16},{19,... | collective-permute-start | bytes 12296 | tf_op jit(solution)/shard_map/ppermute | solution.py:20
  184.7 1.3 fusion.34
  186.0 1.3 fusion.29
  188.8 0.3 fusion.6
  189.1 1.1 fusion.7
  (62 shorter events, 3.3 us)
Async XLA Ops:
  6.5 1.1 copy-start
  6.5 61.6 %all-gather.4.cloned.1.call-start = ((), (), s32[]{:S(2)}) async-start(), calls=%async_computation | async-start | bytes 5013504 | tf_op jit(solution)/shard_map/all_gather | solution.py:52
  8.4 69.8 %copy-start.3 = (f32[512]{0:T(512)S(1)}, f32[512]{0:T(512)}, u32[]{:S(2)}) copy-start(f32[512]{0:T(512)} %param.15) | copy-start | bytes 6148
  8.4 115.0 %all-gather.6.cloned.1.call-start = ((), (), s32[]{:S(2)}) async-start(), calls=%async_computation.1 | async-start | bytes 5013504 | tf_op jit(solution)/shard_map/all_gather | solution.py:52
  10.2 168.6 %all-gather.8.cloned.1.call-start = ((), (), s32[]{:S(2)}) async-start(), calls=%async_computation.2 | async-start | bytes 5013504 | tf_op jit(solution)/shard_map/all_gather | solution.py:52
  11.9 98.5 %copy-start.4 = (f32[512]{0:T(512)S(1)}, f32[512]{0:T(512)}, u32[]{:S(2)}) copy-start(f32[512]{0:T(512)} %param.17) | copy-start | bytes 6148
  11.9 98.5 %copy-start.5 = (f32[512]{0:T(512)S(1)}, f32[512]{0:T(512)}, u32[]{:S(2)}) copy-start(f32[512]{0:T(512)} %param.16) | copy-start | bytes 6148
  45.6 4.4 %collective-permute-start = (bf16[1,64,512]{2,1,0:T(8,128)(2,1)S(1)}, bf16[1,64,512]{2,1,0:T(8,128)(2,1)S(1)}, u32[]{:S(2)}, u32[]{:S(2)}) collective-permute-start(bf16[1,64,512]{2,1,0:T(8,128)(2,1)S(1)} %fusion.69), channel_id=1, source_target_pairs={{0,2},{2,4},{4,6},{6,8},{8,10},{10,12},{12,14},{1,3},{3,5},{5,7},{... | collective-permute-start | bytes 196616 | tf_op jit(solution)/shard_map/ppermute | solution.py:18
  46.9 6.9 %collective-permute-start.1 = (bf16[1,64,512]{2,1,0:T(8,128)(2,1)S(1)}, bf16[1,64,512]{2,1,0:T(8,128)(2,1)S(1)}, u32[]{:S(2)}, u32[]{:S(2)}) collective-permute-start(bf16[1,64,512]{2,1,0:T(8,128)(2,1)S(1)} %fusion.69), channel_id=1, source_target_pairs={{2,0},{4,2},{6,4},{8,6},{10,8},{12,10},{14,12},{3,1},{5,3},{7,5},{... | collective-permute-start | bytes 196616 | tf_op jit(solution)/shard_map/ppermute | solution.py:20
  53.9 6.9 %collective-permute-start.2 = (bf16[3,1,512]{2,1,0:T(2,128)(2,1)S(1)}, bf16[3,1,512]{2,1,0:T(2,128)(2,1)S(1)}, u32[]{:S(2)}, u32[]{:S(2)}) collective-permute-start(bf16[3,1,512]{2,1,0:T(2,128)(2,1)S(1)} %get-tuple-element.19), channel_id=1, source_target_pairs={{0,1},{2,3},{4,5},{6,7},{8,9},{10,11},{12,13},{14,15},{16,17},{18,... | collective-permute-start | bytes 9224 | tf_op jit(solution)/shard_map/ppermute | solution.py:18
  55.2 15.4 %collective-permute-start.3 = (bf16[3,1,512]{2,1,0:T(2,128)(2,1)S(1)}, bf16[3,1,512]{2,1,0:T(2,128)(2,1)S(1)}, u32[]{:S(2)}, u32[]{:S(2)}) collective-permute-start(bf16[3,1,512]{2,1,0:T(2,128)(2,1)S(1)} %get-tuple-element.20), channel_id=1, source_target_pairs={{1,0},{3,2},{5,4},{7,6},{9,8},{11,10},{13,12},{15,14},{17,16},{19,... | collective-permute-start | bytes 9224 | tf_op jit(solution)/shard_map/ppermute | solution.py:20
  78.2 58.8 %copy-start.2 = (bf16[1,64,512]{2,1,0:T(8,128)(2,1)S(1)}, bf16[1,64,512]{2,1,0:T(8,128)(2,1)}, u32[]{:S(2)}) copy-start(bf16[1,64,512]{2,1,0:T(8,128)(2,1)} %param.11) | copy-start | bytes 196612
  78.2 58.8 %copy-start.6 = (f32[512]{0:T(512)S(1)}, f32[512]{0:T(512)}, u32[]{:S(2)}) copy-start(f32[512]{0:T(512)} %param.19) | copy-start | bytes 6148
  110.5 14.2 %collective-permute-start.4 = (bf16[1,64,512]{2,1,0:T(8,128)(2,1)S(1)}, bf16[1,64,512]{2,1,0:T(8,128)(2,1)S(1)}, u32[]{:S(2)}, u32[]{:S(2)}) collective-permute-start(bf16[1,64,512]{2,1,0:T(8,128)(2,1)S(1)} %fusion.153), channel_id=1, source_target_pairs={{0,2},{2,4},{4,6},{6,8},{8,10},{10,12},{12,14},{1,3},{3,5},{5,7},{... | collective-permute-start | bytes 196616 | tf_op jit(solution)/shard_map/ppermute | solution.py:18
  111.8 12.9 %collective-permute-start.5 = (bf16[1,64,512]{2,1,0:T(8,128)(2,1)S(1)}, bf16[1,64,512]{2,1,0:T(8,128)(2,1)S(1)}, u32[]{:S(2)}, u32[]{:S(2)}) collective-permute-start(bf16[1,64,512]{2,1,0:T(8,128)(2,1)S(1)} %fusion.153), channel_id=1, source_target_pairs={{2,0},{4,2},{6,4},{8,6},{10,8},{12,10},{14,12},{3,1},{5,3},{7,5},{... | collective-permute-start | bytes 196616 | tf_op jit(solution)/shard_map/ppermute | solution.py:20
  124.7 8.5 %collective-permute-start.7 = (bf16[3,1,512]{2,1,0:T(2,128)(2,1)S(1)}, bf16[3,1,512]{2,1,0:T(2,128)(2,1)S(1)}, u32[]{:S(2)}, u32[]{:S(2)}) collective-permute-start(bf16[3,1,512]{2,1,0:T(2,128)(2,1)S(1)} %get-tuple-element.18), channel_id=1, source_target_pairs={{1,0},{3,2},{5,4},{7,6},{9,8},{11,10},{13,12},{15,14},{17,16},{19,... | collective-permute-start | bytes 9224 | tf_op jit(solution)/shard_map/ppermute | solution.py:20
  126.9 3.8 %collective-permute-start.6 = (bf16[3,1,512]{2,1,0:T(2,128)(2,1)S(1)}, bf16[3,1,512]{2,1,0:T(2,128)(2,1)S(1)}, u32[]{:S(2)}, u32[]{:S(2)}) collective-permute-start(bf16[3,1,512]{2,1,0:T(2,128)(2,1)S(1)} %get-tuple-element.17), channel_id=1, source_target_pairs={{0,1},{2,3},{4,5},{6,7},{8,9},{10,11},{12,13},{14,15},{16,17},{18,... | collective-permute-start | bytes 9224 | tf_op jit(solution)/shard_map/ppermute | solution.py:18
  138.5 41.7 %collective-permute-start.8 = (bf16[1,128,512]{2,1,0:T(8,128)(2,1)S(1)}, bf16[1,128,512]{2,1,0:T(8,128)(2,1)S(1)}, u32[]{:S(2)}, u32[]{:S(2)}) collective-permute-start(bf16[1,128,512]{2,1,0:T(8,128)(2,1)S(1)} %slice.150), channel_id=1, source_target_pairs={{0,2},{2,4},{4,6},{6,8},{8,10},{10,12},{12,14},{1,3},{3,5},{5,7},{... | collective-permute-start | bytes 393224 | tf_op jit(solution)/shard_map/ppermute | solution.py:18
  140.9 39.3 %collective-permute-start.9 = (bf16[1,128,512]{2,1,0:T(8,128)(2,1)S(1)}, bf16[1,128,512]{2,1,0:T(8,128)(2,1)S(1)}, u32[]{:S(2)}, u32[]{:S(2)}) collective-permute-start(bf16[1,128,512]{2,1,0:T(8,128)(2,1)S(1)} %slice.150), channel_id=1, source_target_pairs={{2,0},{4,2},{6,4},{8,6},{10,8},{12,10},{14,12},{3,1},{5,3},{7,5},{... | collective-permute-start | bytes 393224 | tf_op jit(solution)/shard_map/ppermute | solution.py:20
  178.8 8.8 %copy-start.1 = (bf16[3,3,512,512]{3,2,1,0:T(8,128)(2,1)S(1)}, bf16[3,3,512,512]{3,2,1,0:T(8,128)(2,1)}, u32[]{:S(2)}) copy-start(bf16[3,3,512,512]{3,2,1,0:T(8,128)(2,1)} %all-gather.8.cloned.1.call-done) | copy-start | bytes 14155780
  180.3 7.0 %collective-permute-start.10 = (bf16[4,1,512]{2,1,0:T(2,128)(2,1)S(1)}, bf16[4,1,512]{2,1,0:T(2,128)(2,1)S(1)}, u32[]{:S(2)}, u32[]{:S(2)}) collective-permute-start(bf16[4,1,512]{2,1,0:T(2,128)(2,1)S(1)} %get-tuple-element.15), channel_id=1, source_target_pairs={{0,1},{2,3},{4,5},{6,7},{8,9},{10,11},{12,13},{14,15},{16,17},{18,... | collective-permute-start | bytes 12296 | tf_op jit(solution)/shard_map/ppermute | solution.py:18
  181.6 5.7 %collective-permute-start.11 = (bf16[4,1,512]{2,1,0:T(2,128)(2,1)S(1)}, bf16[4,1,512]{2,1,0:T(2,128)(2,1)S(1)}, u32[]{:S(2)}, u32[]{:S(2)}) collective-permute-start(bf16[4,1,512]{2,1,0:T(2,128)(2,1)S(1)} %get-tuple-element.16), channel_id=1, source_target_pairs={{1,0},{3,2},{5,4},{7,6},{9,8},{11,10},{13,12},{15,14},{17,16},{19,... | collective-permute-start | bytes 12296 | tf_op jit(solution)/shard_map/ppermute | solution.py:20
  187.5 1.6 copy-start.7
Sparse Core Ops, SparseCore 0:
  9.5 58.5 all-gather.3
  70.3 53.0 all-gather.5
  125.6 53.0 all-gather.7
where the time goes:
time: 198 us; the launch traced here: 197 us
  blocking collectives  61.3 us (31%)
  waiting for transfers between devices  59.9 us (30%)
  matrix products  29.3 us (15%)
  starting transfers between devices  23.6 us (12%)
  between operations  13.6 us (7%)
  local copies, waits for them, and re-layouts  6.39 us (3%)
  other arithmetic  2.58 us (1%)
    psum x2, blocking collectives, norm_silu(): total, squares = lax.psum((total, squares), ('row', 'col'))  61.3 us
    all_gather x3, waiting for transfers between devices, convolve(): piece = lax.all_gather(own, ('row', 'col'), axis=2, tiled=True)  54.2 us
    dot_general x27, matrix products, convolve(): jnp.einsum('hwk,kc->hwc', window, piece[offset_y, offset_x], preferred_el...  29.3 us
    ppermute x6, starting transfers between devices, extended(): lax.ppermute(head, axis, [((i + 1) % count, i) for i in range(ends)])  14.6 us
    ppermute x6, starting transfers between devices, extended(): lax.ppermute(tail, axis, [(i, (i + 1) % count) for i in range(ends)])  8.86 us
    dynamic_slice x3, local copies, waits for them, and re-layouts, convolve(): lax.dynamic_slice_in_dim(weight, lax.axis_index('col') * share, share, 2)  4.17 us
  transfers between devices with their start and end apart: 15, of which 5 were waited for; matrix products, arithmetic and copies ran while one was open for 17% of the time, Pallas kernels for 0%

commit v1 on v0

--- a/solution.py
+++ b/solution.py
@@ -5,6 +5,11 @@
 
 G = 32
 EPS = 1e-06
+
+
+def review_samples_all(z, chip_axis):
+    then = jnp.concatenate(lax.all_gather(z, chip_axis), axis=2)
+    return then
 
 
 def extended(cells, sides, width):
@@ -49,7 +54,7 @@
     share = weight.shape[2] // lax.axis_size("col")
     own = lax.dynamic_slice_in_dim(weight, lax.axis_index("col") * share, share, 2)
     total = empty
-    piece = lax.all_gather(own, ("row", "col"), axis=2, tiled=True)
+    piece = review_samples_all(own, ("row", "col"))
     depth = piece.shape[2]
     offset = jnp.asarray(jnp.int32(0), jnp.int32)
     for offset_y in range(3):

time: 198 us -> 220 us (1.11)
  waiting for transfers between devices: 59.9 us -> 87.2 us
  matrix products: 29.3 us -> 11.5 us
  local copies, waits for them, and re-layouts: 6.39 us -> 19.5 us
    all_gather x3, waiting for transfers between devices: 54.2 us -> 75.5 us  [review_samples_all(): then = jnp.concatenate(lax.all_gather(z, chip_axis), axis=2)]
    dot_general x27, matrix products: 29.3 us -> 11.5 us  [convolve(): jnp.einsum('hwk,kc->hwc', window, piece[offset_y, offset_x], preferred_el...]
    reshape x0 -> x2, local copies, waits for them, and re-layouts: none -> 5.47 us  [review_samples_all(): then = jnp.concatenate(lax.all_gather(z, chip_axis), axis=2)]
    all_gather x0 -> x1, local copies, waits for them, and re-layouts: none -> 5.42 us  [review_samples_all(): then = jnp.concatenate(lax.all_gather(z, chip_axis), axis=2)]
    ppermute x6, waiting for transfers between devices: 3.89 us -> 8.53 us  [extended(): lax.ppermute(head, axis, [((i + 1) % count, i) for i in range(ends)])]
  transfers between devices with their start and end apart: 15 -> 15, of which waited for: 5 -> 7; matrix products, arithmetic and copies ran while one was open for 17% -> 11% of each run, Pallas kernels for 0% -> 0%
where the time goes in v1:
time: 220 us; the launch traced here: 219 us
  waiting for transfers between devices  87.2 us (40%)
  blocking collectives  60.9 us (28%)
  starting transfers between devices  23.3 us (11%)
  local copies, waits for them, and re-layouts  19.5 us (9%)
  between operations  13.7 us (6%)
  matrix products  11.5 us (5%)
  other arithmetic  2.58 us (1%)
    all_gather x3, waiting for transfers between devices, review_samples_all(): then = jnp.concatenate(lax.all_gather(z, chip_axis), axis=2)  75.5 us
    psum x2, blocking collectives, norm_silu(): total, squares = lax.psum((total, squares), ('row', 'col'))  60.9 us
    ppermute x6, starting transfers between devices, extended(): lax.ppermute(head, axis, [((i + 1) % count, i) for i in range(ends)])  14.5 us
    dot_general x27, matrix products, convolve(): jnp.einsum('hwk,kc->hwc', window, piece[offset_y, offset_x], preferred_el...  11.5 us
    ppermute x6, starting transfers between devices, extended(): lax.ppermute(tail, axis, [(i, (i + 1) % count) for i in range(ends)])  8.66 us
    ppermute x6, waiting for transfers between devices, extended(): lax.ppermute(head, axis, [((i + 1) % count, i) for i in range(ends)])  8.53 us
    reshape x2, local copies, waits for them, and re-layouts, review_samples_all(): then = jnp.concatenate(lax.all_gather(z, chip_axis), axis=2)  5.47 us
    all_gather x1, local copies, waits for them, and re-layouts, review_samples_all(): then = jnp.concatenate(lax.all_gather(z, chip_axis), axis=2)  5.42 us
  transfers between devices with their start and end apart: 15, of which 7 were waited for; matrix products, arithmetic and copies ran while one was open for 11% of the time, Pallas kernels for 0%

profile of v1, /device:TPU:1, one launch (start us, length us, event | category | flops | bytes accessed | tf_op | source)
XLA Modules:
  0.0 218.6 jit_solution(13874784099330051905)
XLA Ops:
  6.5 1.1 copy-done
  7.6 0.7 constant_dynamic-slice_fusion.2
  8.4 1.7 constant_dynamic-slice_fusion.1
  10.2 1.7 constant_dynamic-slice_fusion
  11.9 0.9 convert_reduce_fusion
  13.2 31.2 %all-reduce.1 = (f32[32]{0:T(128)S(1)}, f32[32]{0:T(128)S(1)}) all-reduce(f32[32]{0:T(128)S(1)} %reduce_sum.54, f32[32]{0:T(128)S(1)} %reduce_sum.51), channel_id=1, replica_groups=mesh['img'=2,'row'=8,'col'=2] {'row','col'}, use_global_device_ids=true, to_apply=%region_5.6 | all-reduce | flops 64 | bytes 512 | tf_op jit(solution)/shard_map/psum | solution.py:37
  44.7 0.9 fusion.69
  45.7 1.3 collective-permute-start
  47.0 1.3 collective-permute-start.1
  48.3 1.8 collective-permute-done
  50.1 3.9 %collective-permute-done.1 = bf16[1,64,512]{2,1,0:T(8,128)(2,1)S(1)} collective-permute-done((bf16[1,64,512]{2,1,0:T(8,128)(2,1)S(1)}, bf16[1,64,512]{2,1,0:T(8,128)(2,1)S(1)}, u32[]{:S(2)}, u32[]{:S(2)}) %collective-permute-start.1) | collective-permute-done | bytes 65568 | tf_op jit(solution)/shard_map/ppermute | solution.py:25
  53.9 5.5 %collective-permute-start.3 = (bf16[3,1,512]{2,1,0:T(2,128)(2,1)S(1)}, bf16[3,1,512]{2,1,0:T(2,128)(2,1)S(1)}, u32[]{:S(2)}, u32[]{:S(2)}) collective-permute-start(bf16[3,1,512]{2,1,0:T(2,128)(2,1)S(1)} %get-tuple-element.20), channel_id=1, source_target_pairs={{1,0},{3,2},{5,4},{7,6},{9,8},{11,10},{13,12},{15,14},{17,16},{19,... | collective-permute-start | bytes 9224 | tf_op jit(solution)/shard_map/ppermute | solution.py:25
  59.4 1.3 collective-permute-start.2
  60.7 7.5 %all-gather.7.cloned.1.call-done = bf16[48,3,32,512]{3,2,1,0:T(8,128)(2,1)} async-done(((bf16[3,3,32,512]{3,2,1,0:T(8,128)(2,1)}), bf16[48,3,32,512]{3,2,1,0:T(8,128)(2,1)}) %all-gather.7.cloned.1.call-update) | async-done | bytes 4718608 | tf_op jit(solution)/shard_map/all_gather | solution.py:11
  68.2 2.7 %copy.17 = bf16[3,3,16,32,512]{4,3,2,1,0:T(8,128)(2,1)S(1)} copy(bf16[3,3,16,32,512]{4,3,1,0,2:T(8,128)(2,1)} %bitcast.210) | data formatting | bytes 9437184 | tf_op jit(solution)/shard_map/reshape | solution.py:11
  71.2 0.2 fusion.42
  71.4 0.2 fusion.46
  71.6 0.2 fusion.44
  72.5 0.2 fusion.19
  72.7 0.2 fusion.151
  73.4 29.7 %all-reduce = (f32[32]{0:T(128)S(1)}, f32[32]{0:T(128)S(1)}) all-reduce(f32[32]{0:T(128)S(1)} %reduce_sum.75, f32[32]{0:T(128)S(1)} %reduce_sum.72), channel_id=1, replica_groups=mesh['img'=2,'row'=8,'col'=2] {'row','col'}, use_global_device_ids=true, to_apply=%region_11.12 | all-reduce | flops 64 | bytes 512 | tf_op jit(solution)/shard_map/psum | solution.py:37
  103.4 1.3 collective-permute-start.4
  104.7 1.3 collective-permute-start.5
  106.0 19.2 %all-gather.9.cloned.1.call-done = bf16[48,3,32,512]{3,2,1,0:T(8,128)(2,1)} async-done(((bf16[3,3,32,512]{3,2,1,0:T(8,128)(2,1)}), bf16[48,3,32,512]{3,2,1,0:T(8,128)(2,1)}) %all-gather.9.cloned.1.call-update) | async-done | bytes 4718608 | tf_op jit(solution)/shard_map/all_gather | solution.py:11
  125.2 2.7 %copy.18 = bf16[3,3,16,32,512]{4,3,2,1,0:T(8,128)(2,1)S(1)} copy(bf16[3,3,16,32,512]{4,3,1,0,2:T(8,128)(2,1)} %bitcast.208) | data formatting | bytes 9437184 | tf_op jit(solution)/shard_map/reshape | solution.py:11
  127.9 2.2 copy-done.1
  130.3 48.9 %all-gather.11.cloned.1.call-done = bf16[48,3,32,512]{3,2,1,0:T(8,128)(2,1)} async-done(((bf16[3,3,32,512]{3,2,1,0:T(8,128)(2,1)}), bf16[48,3,32,512]{3,2,1,0:T(8,128)(2,1)}) %all-gather.11.cloned.1.call-update) | async-done | bytes 4718608 | tf_op jit(solution)/shard_map/all_gather | solution.py:11
  179.2 5.4 %copy.19 = bf16[16,3,3,32,512]{4,3,0,2,1:T(8,128)(2,1)} copy(bf16[16,3,3,32,512]{4,3,2,1,0:T(8,128)(2,1)} %bitcast.209) | data formatting | bytes 9437184 | tf_op jit(solution)/shard_map/all_gather | solution.py:11
  184.6 2.2 collective-permute-start.7
  186.8 1.3 collective-permute-start.6
  188.5 1.3 collective-permute-done.6
  189.9 0.2 fusion.39
  190.7 0.2 fusion.13
  191.0 0.2 fusion.27
  191.4 2.2 %collective-permute-start.8 = (bf16[1,128,512]{2,1,0:T(8,128)(2,1)S(1)}, bf16[1,128,512]{2,1,0:T(8,128)(2,1)S(1)}, u32[]{:S(2)}, u32[]{:S(2)}) collective-permute-start(bf16[1,128,512]{2,1,0:T(8,128)(2,1)S(1)} %slice.150), channel_id=1, source_target_pairs={{0,2},{2,4},{4,6},{6,8},{8,10},{10,12},{12,14},{1,3},{3,5},{5,7},{... | collective-permute-start | bytes 393224 | tf_op jit(solution)/shard_map/ppermute | solution.py:23
  193.6 1.3 collective-permute-start.9
  194.9 1.5 fusion.31
  196.4 4.6 %collective-permute-done.9 = bf16[1,128,512]{2,1,0:T(8,128)(2,1)S(1)} collective-permute-done((bf16[1,128,512]{2,1,0:T(8,128)(2,1)S(1)}, bf16[1,128,512]{2,1,0:T(8,128)(2,1)S(1)}, u32[]{:S(2)}, u32[]{:S(2)}) %collective-permute-start.9) | collective-permute-done | bytes 131104 | tf_op jit(solution)/shard_map/ppermute | solution.py:25
  201.1 1.3 collective-permute-start.10
  202.4 3.0 %collective-permute-start.11 = (bf16[4,1,512]{2,1,0:T(2,128)(2,1)S(1)}, bf16[4,1,512]{2,1,0:T(2,128)(2,1)S(1)}, u32[]{:S(2)}, u32[]{:S(2)}) collective-permute-start(bf16[4,1,512]{2,1,0:T(2,128)(2,1)S(1)} %get-tuple-element.16), channel_id=1, source_target_pairs={{1,0},{3,2},{5,4},{7,6},{9,8},{11,10},{13,12},{15,14},{17,16},{19,... | collective-permute-start | bytes 12296 | tf_op jit(solution)/shard_map/ppermute | solution.py:25
  205.5 1.3 fusion.34
  206.8 1.3 fusion.29
  208.4 1.3 fusion.32
  209.7 0.3 fusion.30
  210.0 0.3 fusion.33
  210.3 0.3 fusion.28
  210.7 0.3 fusion.6
  211.0 1.0 fusion.7
  (72 shorter events, 4.1 us)
Async XLA Ops:
  6.5 1.1 copy-start
  6.5 61.6 %all-gather.7.cloned.1.call-start = ((), (), s32[]{:S(2)}) async-start(), calls=%async_computation | async-start | bytes 5013504 | tf_op jit(solution)/shard_map/all_gather | solution.py:11
  8.4 116.8 %all-gather.9.cloned.1.call-start = ((), (), s32[]{:S(2)}) async-start(), calls=%async_computation.1 | async-start | bytes 5013504 | tf_op jit(solution)/shard_map/all_gather | solution.py:11
  10.2 169.0 %all-gather.11.cloned.1.call-start = ((), (), s32[]{:S(2)}) async-start(), calls=%async_computation.2 | async-start | bytes 5013504 | tf_op jit(solution)/shard_map/all_gather | solution.py:11
  45.7 4.4 %collective-permute-start = (bf16[1,64,512]{2,1,0:T(8,128)(2,1)S(1)}, bf16[1,64,512]{2,1,0:T(8,128)(2,1)S(1)}, u32[]{:S(2)}, u32[]{:S(2)}) collective-permute-start(bf16[1,64,512]{2,1,0:T(8,128)(2,1)S(1)} %fusion.69), channel_id=1, source_target_pairs={{0,2},{2,4},{4,6},{6,8},{8,10},{10,12},{12,14},{1,3},{3,5},{5,7},{... | collective-permute-start | bytes 196616 | tf_op jit(solution)/shard_map/ppermute | solution.py:23
  47.0 6.9 %collective-permute-start.1 = (bf16[1,64,512]{2,1,0:T(8,128)(2,1)S(1)}, bf16[1,64,512]{2,1,0:T(8,128)(2,1)S(1)}, u32[]{:S(2)}, u32[]{:S(2)}) collective-permute-start(bf16[1,64,512]{2,1,0:T(8,128)(2,1)S(1)} %fusion.69), channel_id=1, source_target_pairs={{2,0},{4,2},{6,4},{8,6},{10,8},{12,10},{14,12},{3,1},{5,3},{7,5},{... | collective-permute-start | bytes 196616 | tf_op jit(solution)/shard_map/ppermute | solution.py:25
  53.9 17.0 %collective-permute-start.3 = (bf16[3,1,512]{2,1,0:T(2,128)(2,1)S(1)}, bf16[3,1,512]{2,1,0:T(2,128)(2,1)S(1)}, u32[]{:S(2)}, u32[]{:S(2)}) collective-permute-start(bf16[3,1,512]{2,1,0:T(2,128)(2,1)S(1)} %get-tuple-element.20), channel_id=1, source_target_pairs={{1,0},{3,2},{5,4},{7,6},{9,8},{11,10},{13,12},{15,14},{17,16},{19,... | collective-permute-start | bytes 9224 | tf_op jit(solution)/shard_map/ppermute | solution.py:25
  59.4 12.0 %collective-permute-start.2 = (bf16[3,1,512]{2,1,0:T(2,128)(2,1)S(1)}, bf16[3,1,512]{2,1,0:T(2,128)(2,1)S(1)}, u32[]{:S(2)}, u32[]{:S(2)}) collective-permute-start(bf16[3,1,512]{2,1,0:T(2,128)(2,1)S(1)} %get-tuple-element.19), channel_id=1, source_target_pairs={{0,1},{2,3},{4,5},{6,7},{8,9},{10,11},{12,13},{14,15},{16,17},{18,... | collective-permute-start | bytes 9224 | tf_op jit(solution)/shard_map/ppermute | solution.py:23
  70.9 1.8 copy-start.4
  70.9 32.4 %copy-start.5 = (f32[512]{0:T(512)S(1)}, f32[512]{0:T(512)}, u32[]{:S(2)}) copy-start(f32[512]{0:T(512)} %param.17) | copy-start | bytes 6148
  70.9 32.4 %copy-start.6 = (f32[512]{0:T(512)S(1)}, f32[512]{0:T(512)}, u32[]{:S(2)}) copy-start(f32[512]{0:T(512)} %param.16) | copy-start | bytes 6148
  103.4 81.2 %collective-permute-start.4 = (bf16[1,64,512]{2,1,0:T(8,128)(2,1)S(1)}, bf16[1,64,512]{2,1,0:T(8,128)(2,1)S(1)}, u32[]{:S(2)}, u32[]{:S(2)}) collective-permute-start(bf16[1,64,512]{2,1,0:T(8,128)(2,1)S(1)} %fusion.153), channel_id=1, source_target_pairs={{0,2},{2,4},{4,6},{6,8},{8,10},{10,12},{12,14},{1,3},{3,5},{5,7},{... | collective-permute-start | bytes 196616 | tf_op jit(solution)/shard_map/ppermute | solution.py:23
  104.7 79.9 %collective-permute-start.5 = (bf16[1,64,512]{2,1,0:T(8,128)(2,1)S(1)}, bf16[1,64,512]{2,1,0:T(8,128)(2,1)S(1)}, u32[]{:S(2)}, u32[]{:S(2)}) collective-permute-start(bf16[1,64,512]{2,1,0:T(8,128)(2,1)S(1)} %fusion.153), channel_id=1, source_target_pairs={{2,0},{4,2},{6,4},{8,6},{10,8},{12,10},{14,12},{3,1},{5,3},{7,5},{... | collective-permute-start | bytes 196616 | tf_op jit(solution)/shard_map/ppermute | solution.py:25
  127.9 2.2 %copy-start.1 = (bf16[3,3,16,32,512]{4,3,2,1,0:T(8,128)(2,1)}, bf16[3,3,16,32,512]{4,3,2,1,0:T(8,128)(2,1)S(1)}, u32[]{:S(2)}) copy-start(bf16[3,3,16,32,512]{4,3,2,1,0:T(8,128)(2,1)S(1)} %copy.18) | copy-start | bytes 14155780
  179.2 8.9 %copy-start.2 = (bf16[3,3,16,32,512]{4,3,2,1,0:T(8,128)(2,1)S(1)}, bf16[3,3,16,32,512]{4,3,2,1,0:T(8,128)(2,1)}, u32[]{:S(2)}) copy-start(bf16[3,3,16,32,512]{4,3,2,1,0:T(8,128)(2,1)} %copy-done.1) | copy-start | bytes 14155780
  184.6 6.4 %copy-start.3 = (bf16[1,64,512]{2,1,0:T(8,128)(2,1)S(1)}, bf16[1,64,512]{2,1,0:T(8,128)(2,1)}, u32[]{:S(2)}) copy-start(bf16[1,64,512]{2,1,0:T(8,128)(2,1)} %param.11) | copy-start | bytes 196612
  184.6 6.4 %copy-start.7 = (f32[512]{0:T(512)S(1)}, f32[512]{0:T(512)}, u32[]{:S(2)}) copy-start(f32[512]{0:T(512)} %param.19) | copy-start | bytes 6148
  184.6 5.7 %collective-permute-start.7 = (bf16[3,1,512]{2,1,0:T(2,128)(2,1)S(1)}, bf16[3,1,512]{2,1,0:T(2,128)(2,1)S(1)}, u32[]{:S(2)}, u32[]{:S(2)}) collective-permute-start(bf16[3,1,512]{2,1,0:T(2,128)(2,1)S(1)} %get-tuple-element.18), channel_id=1, source_target_pairs={{1,0},{3,2},{5,4},{7,6},{9,8},{11,10},{13,12},{15,14},{17,16},{19,... | collective-permute-start | bytes 9224 | tf_op jit(solution)/shard_map/ppermute | solution.py:25
  186.8 3.1 %collective-permute-start.6 = (bf16[3,1,512]{2,1,0:T(2,128)(2,1)S(1)}, bf16[3,1,512]{2,1,0:T(2,128)(2,1)S(1)}, u32[]{:S(2)}, u32[]{:S(2)}) collective-permute-start(bf16[3,1,512]{2,1,0:T(2,128)(2,1)S(1)} %get-tuple-element.17), channel_id=1, source_target_pairs={{0,1},{2,3},{4,5},{6,7},{8,9},{10,11},{12,13},{14,15},{16,17},{18,... | collective-permute-start | bytes 9224 | tf_op jit(solution)/shard_map/ppermute | solution.py:23
  190.1 19.6 %slice-start = ((s8[4718592]{0:T(1024)(128)(4,1)}), s8[524288]{0:T(1024)(128)(4,1)S(1)}, s32[]{:S(2)}) async-start(s8[4718592]{0:T(1024)(128)(4,1)} %bitcast.201), calls=%async_computation.3 | async-start | bytes 1048576
  191.4 5.0 %collective-permute-start.8 = (bf16[1,128,512]{2,1,0:T(8,128)(2,1)S(1)}, bf16[1,128,512]{2,1,0:T(8,128)(2,1)S(1)}, u32[]{:S(2)}, u32[]{:S(2)}) collective-permute-start(bf16[1,128,512]{2,1,0:T(8,128)(2,1)S(1)} %slice.150), channel_id=1, source_target_pairs={{0,2},{2,4},{4,6},{6,8},{8,10},{10,12},{12,14},{1,3},{3,5},{5,7},{... | collective-permute-start | bytes 393224 | tf_op jit(solution)/shard_map/ppermute | solution.py:23
  193.6 7.5 %collective-permute-start.9 = (bf16[1,128,512]{2,1,0:T(8,128)(2,1)S(1)}, bf16[1,128,512]{2,1,0:T(8,128)(2,1)S(1)}, u32[]{:S(2)}, u32[]{:S(2)}) collective-permute-start(bf16[1,128,512]{2,1,0:T(8,128)(2,1)S(1)} %slice.150), channel_id=1, source_target_pairs={{2,0},{4,2},{6,4},{8,6},{10,8},{12,10},{14,12},{3,1},{5,3},{7,5},{... | collective-permute-start | bytes 393224 | tf_op jit(solution)/shard_map/ppermute | solution.py:25
  194.9 14.8 %slice-start.1 = ((s8[4718592]{0:T(1024)(128)(4,1)}), s8[4194304]{0:T(1024)(128)(4,1)S(1)}, s32[]{:S(2)}) async-start(s8[4718592]{0:T(1024)(128)(4,1)} %bitcast.201), calls=%async_computation.4 | async-start | bytes 8388608
  201.1 7.0 %collective-permute-start.10 = (bf16[4,1,512]{2,1,0:T(2,128)(2,1)S(1)}, bf16[4,1,512]{2,1,0:T(2,128)(2,1)S(1)}, u32[]{:S(2)}, u32[]{:S(2)}) collective-permute-start(bf16[4,1,512]{2,1,0:T(2,128)(2,1)S(1)} %get-tuple-element.15), channel_id=1, source_target_pairs={{0,1},{2,3},{4,5},{6,7},{8,9},{10,11},{12,13},{14,15},{16,17},{18,... | collective-permute-start | bytes 12296 | tf_op jit(solution)/shard_map/ppermute | solution.py:23
  202.4 5.7 %collective-permute-start.11 = (bf16[4,1,512]{2,1,0:T(2,128)(2,1)S(1)}, bf16[4,1,512]{2,1,0:T(2,128)(2,1)S(1)}, u32[]{:S(2)}, u32[]{:S(2)}) collective-permute-start(bf16[4,1,512]{2,1,0:T(2,128)(2,1)S(1)} %get-tuple-element.16), channel_id=1, source_target_pairs={{1,0},{3,2},{5,4},{7,6},{9,8},{11,10},{13,12},{15,14},{17,16},{19,... | collective-permute-start | bytes 12296 | tf_op jit(solution)/shard_map/ppermute | solution.py:25
  208.3 2.6 %copy-start.8 = (f32[512]{0:T(512)S(1)}, f32[512]{0:T(512)}, u32[]{:S(2)}) copy-start(f32[512]{0:T(512)} %param.21) | copy-start | bytes 6148
Sparse Core Ops, SparseCore 0:
  9.6 58.5 all-gather.6
  70.5 54.6 all-gather.8
  127.5 51.6 all-gather.10
